TPU v7x, 32 devices: a whole 2x2x4 slice. The times are simulated.
32 devices in a mesh: shift: 2 (over y), expert: 4 (over z), shard: 4 (over x, core).
Axes of the slice: x: 2, y: 2, z: 4, core: 2. Of those that a mesh axis runs over, the one named last changes fastest.
Arguments:
- master_gate: float32 [128, 2048, 1024], P(('shift', 'expert'), 'shard'), parts along dimension 0, may hold values from -0.1875 to 0.1875
- master_up: float32 [128, 2048, 1024], P(('shift', 'expert'), 'shard'), parts along dimension 0, may hold values from -0.1875 to 0.1875
- router_weight: float32 [4096, 64], P(('shift', 'shard'), 'expert'), parts along dimension 0, may hold values from -0.125 to 0.125
- router_gain: float32 [4096], P(('shift', 'shard')), parts along dimension 0, may hold values from 0.25 to 1.75
Outputs:
- final_gate: bfloat16 [128, 2048, 1024], P(('shift', 'expert'), None, 'shard'), parts along dimension 0
- final_up: bfloat16 [128, 2048, 1024], P(('shift', 'expert'), None, 'shard'), parts along dimension 0
- scale_gate: float32 [128, 1024], P(('shift', 'expert'), 'shard'), parts along dimension 0
- scale_up: float32 [128, 1024], P(('shift', 'expert'), 'shard'), parts along dimension 0
- serve_router: bfloat16 [4096, 64], P('shift'), parts along dimension 0
There are 2 independent parts, one for each index of `shift`. A program takes and returns all parts, laid end to end along the dimension named above; each array names one. Nothing has to cross between parts.
All inputs are finite; a program needn't handle non-finite values. Where the computation divides by a largest or mean magnitude, that divisor is 1e-20 or more.
Results may differ from a plain program's by a relative error of at most 0.001.
Values may be sent and summed in bfloat16 or wider, within the bound.
No kernel may reach another device: no remote copies, remote signals or barrier semaphores. Data moves between devices by JAX's collectives and lax.ppermute only.
A program may use at most 256 MiB of HBM per device.

v0:
```python
import jax
import jax.numpy as jnp
from jax import lax
from jax.sharding import PartitionSpec as P


def shards(master_gate, master_up, router_weight, router_gain):
    scale_gate, scale_up = lax.pmax(
        (jnp.max(jnp.abs(master_gate), axis=1), jnp.max(jnp.abs(master_up), axis=1)), "shard"
    )
    narrow_gate, narrow_up = (
        (master_gate / jnp.expand_dims(scale_gate, 1)).astype(jnp.bfloat16),
        (master_up / jnp.expand_dims(scale_up, 1)).astype(jnp.bfloat16),
    )
    final_gate, final_up = (
        lax.all_to_all(narrow_gate, "shard", split_axis=2, concat_axis=1, tiled=True),
        lax.all_to_all(narrow_up, "shard", split_axis=2, concat_axis=1, tiled=True),
    )
    scale_gate = lax.dynamic_slice_in_dim(
        scale_gate, lax.axis_index("shard") * final_gate.shape[2], final_gate.shape[2], axis=1
    )
    scale_up = lax.dynamic_slice_in_dim(
        scale_up, lax.axis_index("shard") * final_up.shape[2], final_up.shape[2], axis=1
    )
    part_router = (router_weight * router_gain[:, None]).astype(jnp.bfloat16)
    row_router = lax.all_gather(part_router, "shard", axis=0, tiled=True)
    serve_router = lax.all_gather(row_router, "expert", axis=1, tiled=True)
    return (final_gate, final_up, scale_gate, scale_up, serve_router)


def solution(mesh):
    in_specs = (
        P(("shift", "expert"), "shard", None),
        P(("shift", "expert"), "shard", None),
        P(("shift", "shard"), "expert"),
        P(("shift", "shard")),
    )
    out_specs = (
        P(("shift", "expert"), None, "shard"),
        P(("shift", "expert"), None, "shard"),
        P(("shift", "expert"), "shard"),
        P(("shift", "expert"), "shard"),
        P("shift", None),
    )
    return jax.shard_map(shards, mesh=mesh, in_specs=in_specs, out_specs=out_specs, check_vma=False)
```

profile of v0, /device:TPU:0, one launch (start us, length us, event | category | flops | bytes accessed | tf_op | source)
XLA Modules:
  0.0 541.3 jit_solution(9778503414393642907)
XLA Ops:
  7.2 0.0 all-reduce.3.cloned.1.call-start
  7.2 0.0 copy-start
  7.2 12.6 %abs_reduce_fusion = f32[16,1024]{1,0:T(8,128)} fusion(f32[16,512,1024]{2,1,0:T(8,128)} %param.5), kind=kLoop, calls=%fused_computation.1 | loop fusion | flops 16760832 | bytes 33619968 | tf_op jit(solution)/shard_map/reduce_max | solution.py:9
  19.8 7.6 %copy-done = f32[16,512,1024]{2,1,0:T(8,128)S(1)} copy-done((f32[16,512,1024]{2,1,0:T(8,128)S(1)}, f32[16,512,1024]{2,1,0:T(8,128)}, u32[]{:S(2)}) %copy-start) | copy-done | bytes 33554456
  27.4 2.7 abs_reduce_fusion.1
  30.1 0.0 all-reduce.3.cloned.1.call-update
  30.2 34.2 %copy.12 = f32[16,512,1024]{1,0,2:T(8,128)} copy(f32[16,512,1024]{2,1,0:T(8,128)} %param.4) | data formatting | bytes 67108864 | tf_op args[0]
  64.4 0.5 all-reduce.3.cloned.1.call-done
  64.9 1.0 copy.11
  66.0 17.7 %divide_convert_fusion.1 = bf16[16,512,1024]{1,0,2:T(8,128)(2,1)} fusion(f32[16,512,1024]{1,0,2:T(8,128)} %copy.12, f32[16,1024]{0,1:T(8,128)S(1)} %copy.11), kind=kLoop, calls=%fused_computation.2 | loop fusion | flops 16777216 | bytes 50397184 | tf_op jit(solution)/shard_map/convert_element_type | solution.py:12
  83.6 7.1 %all-to-all-start = ((bf16[16,512,1024]{1,0,2:T(8,128)(2,1)}), bf16[16,512,1024]{1,0,2:T(8,128)(2,1)}, u32[]{:S(2)}, u32[]{:S(2)}) async-start(bf16[16,512,1024]{1,0,2:T(8,128)(2,1)} %divide_convert_fusion.1), calls=%async_computation | async-start | bytes 33554432 | tf_op jit(solution)/shard_map/all_to_all | solution.py:16
  90.7 34.2 %copy.15 = f32[16,512,1024]{1,0,2:T(8,128)} copy(f32[16,512,1024]{2,1,0:T(8,128)} %param.5) | data formatting | bytes 67108864 | tf_op args[1]
  124.9 0.2 copy.14
  125.1 0.0 copy-start.2
  125.1 0.0 copy-start.3
  125.2 17.7 %divide_convert_fusion = bf16[16,512,1024]{1,0,2:T(8,128)(2,1)} fusion(f32[16,512,1024]{1,0,2:T(8,128)} %copy.15, f32[16,1024]{0,1:T(8,128)S(1)} %copy.14), kind=kLoop, calls=%fused_computation | loop fusion | flops 16777216 | bytes 50397184 | tf_op jit(solution)/shard_map/convert_element_type | solution.py:13
  142.8 131.1 %all-to-all-done = bf16[16,512,1024]{1,0,2:T(8,128)(2,1)} async-done(((bf16[16,512,1024]{1,0,2:T(8,128)(2,1)}), bf16[16,512,1024]{1,0,2:T(8,128)(2,1)}, u32[]{:S(2)}, u32[]{:S(2)}) %all-to-all-start) | async-done | bytes 16777248 | tf_op jit(solution)/shard_map/all_to_all | solution.py:16
  273.9 7.0 %all-to-all-start.1 = ((bf16[16,512,1024]{1,0,2:T(8,128)(2,1)}), bf16[16,512,1024]{1,0,2:T(8,128)(2,1)}, u32[]{:S(2)}, u32[]{:S(2)}) async-start(bf16[16,512,1024]{1,0,2:T(8,128)(2,1)} %divide_convert_fusion), calls=%async_computation.1 | async-start | bytes 33554432 | tf_op jit(solution)/shard_map/all_to_all | solution.py:17
  280.9 184.1 %all_gather.6 = bf16[2048,16]{0,1:T(8,128)(2,1)S(1)} all-gather(bf16[512,16]{0,1:T(8,128)(2,1)S(1)} %multiply_convert_fusion), channel_id=1, replica_groups=mesh['shift'=2,'expert'=4,'shard'=4] {'shard'}, dimensions={0}, use_global_device_ids=true | all-gather | bytes 81920 | tf_op jit(solution)/shard_map/all_gather | solution.py:26
  465.0 15.1 %all_gather.7 = bf16[2048,64]{0,1:T(8,128)(2,1)S(1)} all-gather(bf16[2048,16]{0,1:T(8,128)(2,1)S(1)} %all_gather.6), channel_id=1, replica_groups=mesh['shift'=2,'expert'=4,'shard'=4] {'expert'}, dimensions={1}, use_global_device_ids=true | all-gather | bytes 327680 | tf_op jit(solution)/shard_map/all_gather | solution.py:27
  480.1 1.3 constant_dynamic-slice_fusion
  481.4 26.2 %copy.13 = bf16[16,4,512,256]{3,2,1,0:T(8,128)(2,1)} copy(bf16[16,4,512,256]{2,0,3,1:T(8,128)(2,1)} %bitcast.1) | data formatting | bytes 33554432 | tf_op jit(solution)/shard_map/all_to_all | solution.py:16
  507.6 26.2 %copy.16 = bf16[16,4,512,256]{3,2,1,0:T(8,128)(2,1)} copy(bf16[16,4,512,256]{2,0,3,1:T(8,128)(2,1)} %bitcast.4) | data formatting | bytes 33554432 | tf_op jit(solution)/shard_map/all_to_all | solution.py:17
  533.8 0.7 copy.20
  (6 shorter events, 0.0 us)
Async XLA Ops:
  7.2 57.7 %all-reduce.3.cloned.1.call-start = ((), (), s32[]{:S(2)}) async-start(), calls=%async_computation.2 | async-start | bytes 262144 | tf_op jit(solution)/shard_map/pmax | solution.py:8
  7.2 20.2 %copy-start = (f32[16,512,1024]{2,1,0:T(8,128)S(1)}, f32[16,512,1024]{2,1,0:T(8,128)}, u32[]{:S(2)}) copy-start(f32[16,512,1024]{2,1,0:T(8,128)} %param.4) | copy-start | bytes 100663296
  83.6 190.3 %all-to-all-start = ((bf16[16,512,1024]{1,0,2:T(8,128)(2,1)}), bf16[16,512,1024]{1,0,2:T(8,128)(2,1)}, u32[]{:S(2)}, u32[]{:S(2)}) async-start(bf16[16,512,1024]{1,0,2:T(8,128)(2,1)} %divide_convert_fusion.1), calls=%async_computation | async-start | bytes 33554432 | tf_op jit(solution)/shard_map/all_to_all | solution.py:16
  90.7 34.2 %copy-start.1 = (f32[16,1024]{1,0:T(8,128)S(1)}, f32[16,1024]{1,0:T(8,128)}, u32[]{:S(2)}) copy-start(f32[16,1024]{1,0:T(8,128)} %get-tuple-element.6) | copy-start | bytes 196612
  125.1 155.7 %copy-start.2 = (f32[512,16]{0,1:T(8,128)S(1)}, f32[512,16]{0,1:T(8,128)}, u32[]{:S(2)}) copy-start(f32[512,16]{0,1:T(8,128)} %param.6) | copy-start | bytes 98308
  125.1 155.7 %copy-start.3 = (f32[512]{0:T(512)S(1)}, f32[512]{0:T(512)}, u32[]{:S(2)}) copy-start(f32[512]{0:T(512)} %param.7) | copy-start | bytes 6148
  273.9 233.7 %all-to-all-start.1 = ((bf16[16,512,1024]{1,0,2:T(8,128)(2,1)}), bf16[16,512,1024]{1,0,2:T(8,128)(2,1)}, u32[]{:S(2)}, u32[]{:S(2)}) async-start(bf16[16,512,1024]{1,0,2:T(8,128)(2,1)} %divide_convert_fusion), calls=%async_computation.1 | async-start | bytes 33554432 | tf_op jit(solution)/shard_map/all_to_all | solution.py:17
Sparse Core Ops, SparseCore 0:
  30.3 34.5 all-reduce.2
where the time goes:
time: 544 us; the launch traced here: 541 us
  blocking collectives  199 us (37%)
  local copies, waits for them, and re-layouts  132 us (24%)
  waiting for transfers between devices  132 us (24%)
  other arithmetic  50.7 us (9%)
  starting transfers between devices  14.1 us (3%)
  between operations  14.1 us (3%)
    all_gather x1, blocking collectives, shards(): row_router = lax.all_gather(part_router, 'shard', axis=0, tiled=True)  184 us
    all_to_all x1, waiting for transfers between devices, shards(): lax.all_to_all(narrow_gate, 'shard', split_axis=2, concat_axis=1, tiled=T...  131 us
    unnamed x11, local copies, waits for them, and re-layouts  76.7 us
    all_to_all x1, local copies, waits for them, and re-layouts, shards(): lax.all_to_all(narrow_up, 'shard', split_axis=2, concat_axis=1, tiled=True)  26.2 us
    all_to_all x1, local copies, waits for them, and re-layouts, shards(): lax.all_to_all(narrow_gate, 'shard', split_axis=2, concat_axis=1, tiled=T...  26.2 us
    convert_element_type x1, other arithmetic, shards(): (master_gate / jnp.expand_dims(scale_gate, 1)).astype(jnp.bfloat16)  17.7 us
    convert_element_type x1, other arithmetic, shards(): (master_up / jnp.expand_dims(scale_up, 1)).astype(jnp.bfloat16)  17.7 us
    all_gather x1, blocking collectives, shards(): serve_router = lax.all_gather(row_router, 'expert', axis=1, tiled=True)  15.1 us
  transfers between devices with their start and end apart: 3, of which 2 were waited for; matrix products, arithmetic and copies ran while one was open for 21% of the time, Pallas kernels for 0%

commit v1 on v0

--- a/solution.py
+++ b/solution.py
@@ -24,7 +24,7 @@
     )
     part_router = (router_weight * router_gain[:, None]).astype(jnp.bfloat16)
     row_router = lax.all_gather(part_router, "shard", axis=0, tiled=True)
-    serve_router = lax.all_gather(row_router, "expert", axis=1, tiled=True)
+    serve_router = jnp.concatenate(lax.all_gather(row_router, "expert"), axis=1)
     return (final_gate, final_up, scale_gate, scale_up, serve_router)
 
 

time: 544 us -> 544 us (level)
    unnamed x11 -> x10, local copies, waits for them, and re-layouts: 76.7 us -> 76 us
where the time goes in v1:
time: 544 us; the launch traced here: 541 us
  blocking collectives  199 us (37%)
  local copies, waits for them, and re-layouts  132 us (24%)
  waiting for transfers between devices  132 us (24%)
  other arithmetic  50.7 us (9%)
  starting transfers between devices  14.1 us (3%)
  between operations  14.1 us (3%)
    all_gather x1, blocking collectives, shards(): row_router = lax.all_gather(part_router, 'shard', axis=0, tiled=True)  184 us
    all_to_all x1, waiting for transfers between devices, shards(): lax.all_to_all(narrow_gate, 'shard', split_axis=2, concat_axis=1, tiled=T...  131 us
    unnamed x10, local copies, waits for them, and re-layouts  76 us
    all_to_all x1, local copies, waits for them, and re-layouts, shards(): lax.all_to_all(narrow_up, 'shard', split_axis=2, concat_axis=1, tiled=True)  26.2 us
    all_to_all x1, local copies, waits for them, and re-layouts, shards(): lax.all_to_all(narrow_gate, 'shard', split_axis=2, concat_axis=1, tiled=T...  26.2 us
    convert_element_type x1, other arithmetic, shards(): (master_gate / jnp.expand_dims(scale_gate, 1)).astype(jnp.bfloat16)  17.7 us
    convert_element_type x1, other arithmetic, shards(): (master_up / jnp.expand_dims(scale_up, 1)).astype(jnp.bfloat16)  17.7 us
    all_gather x1, blocking collectives, shards(): serve_router = jnp.concatenate(lax.all_gather(row_router, 'expert'), axis=1)  15.1 us
  transfers between devices with their start and end apart: 3, of which 2 were waited for; matrix products, arithmetic and copies ran while one was open for 21% of the time, Pallas kernels for 0%

profile of v1, /device:TPU:0, one launch (start us, length us, event | category | flops | bytes accessed | tf_op | source)
XLA Modules:
  0.0 541.3 jit_solution(6056821258190931910)
XLA Ops:
  7.2 0.0 all-reduce.3.cloned.1.call-start
  7.2 0.0 copy-start
  7.2 12.6 %abs_reduce_fusion = f32[16,1024]{1,0:T(8,128)} fusion(f32[16,512,1024]{2,1,0:T(8,128)} %param.5), kind=kLoop, calls=%fused_computation.1 | loop fusion | flops 16760832 | bytes 33619968 | tf_op jit(solution)/shard_map/reduce_max | solution.py:9
  19.8 7.6 %copy-done = f32[16,512,1024]{2,1,0:T(8,128)S(1)} copy-done((f32[16,512,1024]{2,1,0:T(8,128)S(1)}, f32[16,512,1024]{2,1,0:T(8,128)}, u32[]{:S(2)}) %copy-start) | copy-done | bytes 33554456
  27.4 2.7 abs_reduce_fusion.1
  30.1 0.0 all-reduce.3.cloned.1.call-update
  30.2 34.2 %copy.13 = f32[16,512,1024]{1,0,2:T(8,128)} copy(f32[16,512,1024]{2,1,0:T(8,128)} %param.4) | data formatting | bytes 67108864 | tf_op args[0]
  64.4 0.5 all-reduce.3.cloned.1.call-done
  64.9 1.0 copy.12
  66.0 17.7 %divide_convert_fusion.1 = bf16[16,512,1024]{1,0,2:T(8,128)(2,1)} fusion(f32[16,512,1024]{1,0,2:T(8,128)} %copy.13, f32[16,1024]{0,1:T(8,128)S(1)} %copy.12), kind=kLoop, calls=%fused_computation.2 | loop fusion | flops 16777216 | bytes 50397184 | tf_op jit(solution)/shard_map/convert_element_type | solution.py:12
  83.6 7.1 %all-to-all-start = ((bf16[16,512,1024]{1,0,2:T(8,128)(2,1)}), bf16[16,512,1024]{1,0,2:T(8,128)(2,1)}, u32[]{:S(2)}, u32[]{:S(2)}) async-start(bf16[16,512,1024]{1,0,2:T(8,128)(2,1)} %divide_convert_fusion.1), calls=%async_computation | async-start | bytes 33554432 | tf_op jit(solution)/shard_map/all_to_all | solution.py:16
  90.7 34.2 %copy.16 = f32[16,512,1024]{1,0,2:T(8,128)} copy(f32[16,512,1024]{2,1,0:T(8,128)} %param.5) | data formatting | bytes 67108864 | tf_op args[1]
  124.9 0.2 copy.15
  125.1 0.0 copy-start.2
  125.1 0.0 copy-start.3
  125.2 17.7 %divide_convert_fusion = bf16[16,512,1024]{1,0,2:T(8,128)(2,1)} fusion(f32[16,512,1024]{1,0,2:T(8,128)} %copy.16, f32[16,1024]{0,1:T(8,128)S(1)} %copy.15), kind=kLoop, calls=%fused_computation | loop fusion | flops 16777216 | bytes 50397184 | tf_op jit(solution)/shard_map/convert_element_type | solution.py:13
  142.8 131.1 %all-to-all-done = bf16[16,512,1024]{1,0,2:T(8,128)(2,1)} async-done(((bf16[16,512,1024]{1,0,2:T(8,128)(2,1)}), bf16[16,512,1024]{1,0,2:T(8,128)(2,1)}, u32[]{:S(2)}, u32[]{:S(2)}) %all-to-all-start) | async-done | bytes 16777248 | tf_op jit(solution)/shard_map/all_to_all | solution.py:16
  273.9 7.0 %all-to-all-start.1 = ((bf16[16,512,1024]{1,0,2:T(8,128)(2,1)}), bf16[16,512,1024]{1,0,2:T(8,128)(2,1)}, u32[]{:S(2)}, u32[]{:S(2)}) async-start(bf16[16,512,1024]{1,0,2:T(8,128)(2,1)} %divide_convert_fusion), calls=%async_computation.1 | async-start | bytes 33554432 | tf_op jit(solution)/shard_map/all_to_all | solution.py:17
  280.9 184.1 %all_gather.9 = bf16[2048,16]{0,1:T(8,128)(2,1)S(1)} all-gather(bf16[512,16]{0,1:T(8,128)(2,1)S(1)} %multiply_convert_fusion), channel_id=1, replica_groups=mesh['shift'=2,'expert'=4,'shard'=4] {'shard'}, dimensions={0}, use_global_device_ids=true | all-gather | bytes 81920 | tf_op jit(solution)/shard_map/all_gather | solution.py:26
  465.0 15.1 %all-gather = bf16[8192,16]{0,1:T(8,128)(2,1)S(1)} all-gather(bf16[2048,16]{0,1:T(8,128)(2,1)S(1)} %all_gather.9), channel_id=2, replica_groups=mesh['shift'=2,'expert'=4,'shard'=4] {'expert'}, dimensions={0}, use_global_device_ids=true | all-gather | bytes 327680 | tf_op jit(solution)/shard_map/all_gather | solution.py:27
  480.1 0.7 copy.21
  480.8 1.3 constant_dynamic-slice_fusion
  482.2 26.2 %copy.14 = bf16[16,4,512,256]{3,2,1,0:T(8,128)(2,1)} copy(bf16[16,4,512,256]{2,0,3,1:T(8,128)(2,1)} %bitcast.1) | data formatting | bytes 33554432 | tf_op jit(solution)/shard_map/all_to_all | solution.py:16
  508.3 26.2 %copy.17 = bf16[16,4,512,256]{3,2,1,0:T(8,128)(2,1)} copy(bf16[16,4,512,256]{2,0,3,1:T(8,128)(2,1)} %bitcast.4) | data formatting | bytes 33554432 | tf_op jit(solution)/shard_map/all_to_all | solution.py:17
  (6 shorter events, 0.0 us)
Async XLA Ops:
  7.2 57.7 %all-reduce.3.cloned.1.call-start = ((), (), s32[]{:S(2)}) async-start(), calls=%async_computation.2 | async-start | bytes 262144 | tf_op jit(solution)/shard_map/pmax | solution.py:8
  7.2 20.2 %copy-start = (f32[16,512,1024]{2,1,0:T(8,128)S(1)}, f32[16,512,1024]{2,1,0:T(8,128)}, u32[]{:S(2)}) copy-start(f32[16,512,1024]{2,1,0:T(8,128)} %param.4) | copy-start | bytes 100663296
  83.6 190.3 %all-to-all-start = ((bf16[16,512,1024]{1,0,2:T(8,128)(2,1)}), bf16[16,512,1024]{1,0,2:T(8,128)(2,1)}, u32[]{:S(2)}, u32[]{:S(2)}) async-start(bf16[16,512,1024]{1,0,2:T(8,128)(2,1)} %divide_convert_fusion.1), calls=%async_computation | async-start | bytes 33554432 | tf_op jit(solution)/shard_map/all_to_all | solution.py:16
  90.7 34.2 %copy-start.1 = (f32[16,1024]{1,0:T(8,128)S(1)}, f32[16,1024]{1,0:T(8,128)}, u32[]{:S(2)}) copy-start(f32[16,1024]{1,0:T(8,128)} %get-tuple-element.6) | copy-start | bytes 196612
  125.1 155.7 %copy-start.2 = (f32[512,16]{0,1:T(8,128)S(1)}, f32[512,16]{0,1:T(8,128)}, u32[]{:S(2)}) copy-start(f32[512,16]{0,1:T(8,128)} %param.6) | copy-start | bytes 98308
  125.1 155.7 %copy-start.3 = (f32[512]{0:T(512)S(1)}, f32[512]{0:T(512)}, u32[]{:S(2)}) copy-start(f32[512]{0:T(512)} %param.7) | copy-start | bytes 6148
  273.9 234.4 %all-to-all-start.1 = ((bf16[16,512,1024]{1,0,2:T(8,128)(2,1)}), bf16[16,512,1024]{1,0,2:T(8,128)(2,1)}, u32[]{:S(2)}, u32[]{:S(2)}) async-start(bf16[16,512,1024]{1,0,2:T(8,128)(2,1)} %divide_convert_fusion), calls=%async_computation.1 | async-start | bytes 33554432 | tf_op jit(solution)/shard_map/all_to_all | solution.py:17
Sparse Core Ops, SparseCore 0:
  30.3 34.5 all-reduce.2
